TPU v7x, 32 devices: a whole 2x2x4 slice. The times are simulated.
32 devices in a mesh: section: 16 (over z, y, core), dp: 2 (over x).
Axes of the slice: x: 2, y: 2, z: 4, core: 2. Of those that a mesh axis runs over, the one named last changes fastest.
Arguments:
- layer_in: bfloat16 [16, 256, 5120], P('section', 'dp'), may hold values from -6 to 6
- latent: bfloat16 [16, 256, 384], P('section', 'dp'), may hold values from -6 to 6
- mix_grad: bfloat16 [16, 256, 5120], P('section', 'dp'), may hold values from -0.375 to 0.375
- down_proj: bfloat16 [16, 5120, 384], P('section', 'dp'), may hold values from -0.078125 to 0.078125
- up_proj: bfloat16 [16, 384, 5120], P('section', None, 'dp'), may hold values from -0.3125 to 0.3125
- norm_gain: bfloat16 [16, 5120], P('section', 'dp'), may hold values from 0.5 to 1.5
- mix_weight: float32 [16, 8], P('section'), may hold values from 0.2 to 1
Outputs:
- up_grad: bfloat16 [16, 384, 5120], P('section', None, 'dp')
- down_grad: bfloat16 [16, 5120, 384], P('section', 'dp')
- gain_grad: float32 [16, 5120], P('section', 'dp')
- mixing_grad: float32 [16, 8], P('section')
All inputs are finite; a program needn't handle non-finite values.
Results may differ from a plain program's by a relative error of at most 0.0064.
Values may be sent and summed in bfloat16 or wider, within the bound.
A program may use at most 128 MiB of HBM per device.

v0:
```python
import jax
import jax.numpy as jnp
from jax import lax
from jax.sharding import PartitionSpec as P

MIXES = 8


epsilon = 1e-06
root_coef = 0.7978845608028654


def from_behind(value, axis, steps):
    count = lax.axis_size(axis)
    initial, last = (max(0, -steps), min(count, count - steps))
    return lax.ppermute(value, axis, [(source, source + steps) for source in range(initial, last)])


def gelu_pair(values):
    tangent = jnp.tanh(root_coef * (values + 0.044715 * values * values * values))
    result = 0.5 * values * (1.0 + tangent)
    slopes = 0.5 * (1.0 + tangent) + 0.5 * values * (1.0 - tangent * tangent) * root_coef * (
        1.0 + 3.0 * 0.044715 * values * values
    )
    return (result, slopes)


def local(layer_in, latent, mix_grad, down_proj, up_proj, norm_gain, mix_weight):
    width = layer_in.shape[2]
    own_rows = layer_in.shape[1]
    cols_in, cols_grad = (
        lax.all_to_all(layer_in[0], "dp", split_axis=1, concat_axis=0, tiled=True),
        lax.all_to_all(mix_grad[0], "dp", split_axis=1, concat_axis=0, tiled=True),
    )
    latent_all = lax.all_gather(latent[0], "dp", axis=0, tiled=True)
    inputs = cols_in.astype(jnp.float32)
    partial_sq = jnp.sum(inputs * inputs, axis=1)
    total_sq = lax.psum(partial_sq, "dp")
    inv_rms = lax.rsqrt(total_sq / width + epsilon)[:, None]
    scaled = inputs * inv_rms
    normed = (scaled * norm_gain[0].astype(jnp.float32)).astype(jnp.bfloat16)
    activated, slopes = gelu_pair(latent_all.astype(jnp.float32))
    act_half = activated.astype(jnp.bfloat16)
    up_block = up_proj[0]
    layer_out = inputs + jnp.dot(act_half, up_block, preferred_element_type=jnp.float32)
    weights = mix_weight[0]
    stride = lax.axis_size("section") // MIXES

    def absorb(grad_sum, piece, member):
        values = piece.astype(jnp.float32)
        return (grad_sum + weights[member] * values, jnp.sum(values * layer_out))

    grad_sum, first = absorb(jnp.zeros(inputs.shape, jnp.float32), cols_grad, 0)
    products = [first]
    moving = cols_grad
    for member in range(1, MIXES):
        moving = from_behind(moving, "section", -stride)
        grad_sum, product = absorb(grad_sum, moving, member)
        products.append(product)
    grad_half = grad_sum.astype(jnp.bfloat16)
    up_grad = jnp.einsum(
        "tr,tc->rc", act_half, grad_half, preferred_element_type=jnp.float32
    ).astype(jnp.bfloat16)
    act_partial = jnp.einsum("tc,rc->tr", grad_half, up_block, preferred_element_type=jnp.float32)
    own_part = lax.psum_scatter(act_partial, "dp", scatter_dimension=0, tiled=True)
    own_slopes = lax.dynamic_slice_in_dim(slopes, lax.axis_index("dp") * own_rows, own_rows, 0)
    own_grad = (own_part * own_slopes).astype(jnp.bfloat16)
    latent_grad = lax.all_gather(own_grad, "dp", axis=0, tiled=True)
    mixing = lax.psum(jnp.stack(products), "dp")
    down_grad = jnp.einsum(
        "tc,tr->cr", normed, latent_grad, preferred_element_type=jnp.float32
    ).astype(jnp.bfloat16)
    norm_grad = jnp.einsum(
        "tr,cr->tc", latent_grad, down_proj[0], preferred_element_type=jnp.float32
    )
    gain_grad = jnp.sum(norm_grad * scaled, axis=0)
    return (up_grad[None], down_grad[None], gain_grad[None], mixing[None])


def solution(mesh):
    return jax.shard_map(
        local,
        mesh=mesh,
        in_specs=(
            P("section", "dp", None),
            P("section", "dp", None),
            P("section", "dp", None),
            P("section", "dp", None),
            P("section", None, "dp"),
            P("section", "dp"),
            P("section", None),
        ),
        out_specs=(
            P("section", None, "dp"),
            P("section", "dp", None),
            P("section", "dp"),
            P("section", None),
        ),
        check_vma=False,
    )
```

profile of v0, /device:TPU:0, one launch (start us, length us, event | category | flops | bytes accessed | tf_op | source)
XLA Modules:
  0.0 290.3 jit_solution(9529776096178587440)
XLA Ops:
  7.2 0.0 copy-start
  7.2 3.7 %all_to_all.24 = bf16[128,2,2560]{2,1,0:T(2,128)(2,1)S(1)} reshape(bf16[1,128,5120]{2,1,0:T(8,128)(2,1)} %param.9) | data formatting | bytes 2621440 | tf_op jit(solution)/shard_map/all_to_all | solution.py:33
  10.9 0.1 copy.13
  11.0 20.4 %all_to_all.32 = bf16[128,2,2560]{2,0,1:T(8,128)(2,1)S(1)} all-to-all(bf16[128,2,2560]{2,0,1:T(8,128)(2,1)S(1)} %copy.13), channel_id=1, replica_groups=mesh['section'=16,'dp'=2] {'dp'}, dimensions={1} | all-to-all | bytes 2621440 | tf_op jit(solution)/shard_map/all_to_all | solution.py:33
  31.5 1.2 copy-done.2
  32.6 1.3 collective-permute-start
  33.9 30.2 %collective-permute-done = bf16[256,2560]{1,0:T(8,128)(2,1)S(1)} collective-permute-done((bf16[256,2560]{1,0:T(8,128)(2,1)S(1)}, bf16[256,2560]{1,0:T(8,128)(2,1)S(1)}, u32[]{:S(2)}, u32[]{:S(2)}) %collective-permute-start) | collective-permute-done | bytes 1310752 | tf_op jit(solution)/shard_map/ppermute | solution.py:16
  64.1 1.3 collective-permute-start.1
  65.4 30.2 %collective-permute-done.1 = bf16[256,2560]{1,0:T(8,128)(2,1)S(1)} collective-permute-done((bf16[256,2560]{1,0:T(8,128)(2,1)S(1)}, bf16[256,2560]{1,0:T(8,128)(2,1)S(1)}, u32[]{:S(2)}, u32[]{:S(2)}) %collective-permute-start.1) | collective-permute-done | bytes 1310752 | tf_op jit(solution)/shard_map/ppermute | solution.py:16
  95.6 1.3 collective-permute-start.2
  96.9 29.4 %collective-permute-done.2 = bf16[256,2560]{1,0:T(8,128)(2,1)S(1)} collective-permute-done((bf16[256,2560]{1,0:T(8,128)(2,1)S(1)}, bf16[256,2560]{1,0:T(8,128)(2,1)S(1)}, u32[]{:S(2)}, u32[]{:S(2)}) %collective-permute-start.2) | collective-permute-done | bytes 1310752 | tf_op jit(solution)/shard_map/ppermute | solution.py:16
  126.3 1.3 collective-permute-start.3
  127.6 28.5 %collective-permute-done.3 = bf16[256,2560]{1,0:T(8,128)(2,1)S(1)} collective-permute-done((bf16[256,2560]{1,0:T(8,128)(2,1)S(1)}, bf16[256,2560]{1,0:T(8,128)(2,1)S(1)}, u32[]{:S(2)}, u32[]{:S(2)}) %collective-permute-start.3) | collective-permute-done | bytes 1310752 | tf_op jit(solution)/shard_map/ppermute | solution.py:16
  156.1 1.3 collective-permute-start.4
  157.4 27.8 %collective-permute-done.4 = bf16[256,2560]{1,0:T(8,128)(2,1)} collective-permute-done((bf16[256,2560]{1,0:T(8,128)(2,1)S(1)}, bf16[256,2560]{1,0:T(8,128)(2,1)}, u32[]{:S(2)}, u32[]{:S(2)}) %collective-permute-start.4) | collective-permute-done | bytes 1310752 | tf_op jit(solution)/shard_map/ppermute | solution.py:16
  185.1 1.3 collective-permute-start.5
  186.4 3.6 %all_to_all.28 = bf16[128,2,2560]{2,1,0:T(2,128)(2,1)S(1)} reshape(bf16[1,128,5120]{2,1,0:T(8,128)(2,1)} %param.7) | data formatting | bytes 2621440 | tf_op jit(solution)/shard_map/all_to_all | solution.py:32
  190.0 0.0 copy-start.13
  190.0 0.0 copy-start.14
  190.1 1.2 copy.14
  191.2 3.6 %all-to-all-start.1 = ((bf16[128,2,2560]{2,0,1:T(8,128)(2,1)}), bf16[128,2,2560]{2,0,1:T(8,128)(2,1)S(1)}, u32[]{:S(2)}, u32[]{:S(2)}) async-start(bf16[128,2,2560]{2,0,1:T(8,128)(2,1)} %copy.14), calls=%async_computation.1 | async-start | bytes 2621440 | tf_op jit(solution)/shard_map/all_to_all | solution.py:32
  194.9 0.0 reduce-scatter.2.cloned.1.call-start
  194.9 19.2 %collective-permute-done.5 = bf16[256,2560]{1,0:T(8,128)(2,1)} collective-permute-done((bf16[256,2560]{1,0:T(8,128)(2,1)}, bf16[256,2560]{1,0:T(8,128)(2,1)}, u32[]{:S(2)}, u32[]{:S(2)}) %collective-permute-start.5) | collective-permute-done | bytes 1310752 | tf_op jit(solution)/shard_map/ppermute | solution.py:16
  214.1 1.3 collective-permute-start.6
  215.4 0.7 fusion.35
  216.1 5.5 %all-gather = bf16[1,256,384]{2,1,0:T(8,128)(2,1)S(1)} all-gather(bf16[1,128,384]{2,1,0:T(8,128)(2,1)} %param.8), channel_id=2, replica_groups=mesh['section'=16,'dp'=2] {'dp'}, dimensions={1}, use_global_device_ids=true | all-gather | bytes 294912 | tf_op jit(solution)/shard_map/all_gather | solution.py:35
  221.6 0.8 bitcast_convert_fusion
  222.4 1.1 fusion.27
  223.5 0.0 all-to-all-done.1
  223.5 0.3 convert_element_type.80
  223.8 0.3 multiply_reduce_fusion
  224.2 0.0 copy-start.12
  224.2 0.9 convolution_add_fusion
  225.1 16.5 %collective-permute-done.6 = bf16[256,2560]{1,0:T(8,128)(2,1)} collective-permute-done((bf16[256,2560]{1,0:T(8,128)(2,1)}, bf16[256,2560]{1,0:T(8,128)(2,1)}, u32[]{:S(2)}, u32[]{:S(2)}) %collective-permute-start.6) | collective-permute-done | bytes 1310752 | tf_op jit(solution)/shard_map/ppermute | solution.py:16
  241.7 10.6 %fusion.17 = (f32[]{:T(128)}, f32[]{:T(128)}, f32[]{:T(128)}, f32[]{:T(128)}, f32[]{:T(128)}, /*index=5*/f32[]{:T(128)}, f32[]{:T(128)}, f32[]{:T(128)}, bf16[256,2560]{1,0:T(8,128)(2,1)S(1)}) fusion(f32[256,2560]{1,0:T(8,128)S(1)} %convolution_add_fusion, bf16[256,2560]{1,0:T(8,128)(2,1)} %collective-permute-done.6, ...), kind=kLoop, calls=%fused_computation.37 | loop fusion | flops 26214392 | bytes 14417984 | tf_op jit(solution)/shard_map/reduce_sum | solution.py:51
  252.3 2.0 fusion
  254.4 1.6 fusion.20
  256.0 0.0 reduce-scatter.2.cloned.1.call-update
  256.0 5.0 %stack.35 = f32[8]{0:T(128)S(1)} concatenate(f32[1]{0:T(128)} %bitcast.22, f32[1]{0:T(128)} %bitcast.23, f32[1]{0:T(128)} %bitcast.24, f32[1]{0:T(128)} %bitcast.25, f32[1]{0:T(128)} %bitcast.26, f32[1]{0:T(128)} %bitcast.27, f32[1]{0:T(128)} %bitcast.28, f32[1]{0:T(128)} %bitcast.29), dimensions={0} | concatenate | bytes 64 | tf_op jit(solution)/shard_map/stack | solution.py:69
  261.0 5.4 %all-reduce = (f32[256]{0:T(256)S(1)}, f32[1,8]{1,0:T(1,128)}) all-reduce(f32[256]{0:T(256)S(1)} %bitcast.62, f32[1,8]{1,0:T(1,128)S(1)} %bitcast.63), channel_id=1, replica_groups=mesh['section'=16,'dp'=2] {'dp'}, use_global_device_ids=true, to_apply=%region_1.0 | all-reduce | flops 264 | bytes 2112 | tf_op jit(solution)/shard_map/psum | solution.py:38
  266.5 1.8 bitcast_multiply_fusion
  268.2 3.0 %reduce-scatter.2.cloned.1.call-done = f32[128,384]{1,0:T(8,128)} async-done(((f32[256,384]{1,0:T(8,128)}), f32[128,384]{1,0:T(8,128)}) %reduce-scatter.2.cloned.1.call-update) | async-done | bytes 196624 | tf_op jit(solution)/shard_map/reduce_scatter | solution.py:65
  271.2 1.4 fusion.32
  272.6 0.0 copy-start.4
  272.6 5.4 %all_gather.7 = bf16[256,384]{1,0:T(8,128)(2,1)S(1)} all-gather(bf16[128,384]{1,0:T(8,128)(2,1)S(1)} %fusion.32), channel_id=1, replica_groups=mesh['section'=16,'dp'=2] {'dp'}, dimensions={0}, use_global_device_ids=true | all-gather | bytes 294912 | tf_op jit(solution)/shard_map/all_gather | solution.py:68
  278.0 3.9 %fusion.1 = bf16[1,2560,384]{2,1,0:T(8,128)(2,1)} fusion(bf16[256,384]{1,0:T(8,128)(2,1)S(1)} %all_gather.7, f32[256,2560]{1,0:T(8,128)} %bitcast_multiply_fusion, f32[2560]{0:T(1024)S(1)} %convert_reduce_fusion), kind=kOutput, calls=%fused_computation.5 | convolution fusion | flops 505610240 | bytes 4794368 | tf_op jit(solution)/shard_map/tc,tr->cr/dot_general | solution.py:70
  281.9 0.9 fusion.22
  282.8 0.6 broadcast_in_dim.16
  (26 shorter events, 0.1 us)
Async XLA Ops:
  7.2 217.0 %copy-start = (bf16[1,384,2560]{2,1,0:T(8,128)(2,1)S(1)}, bf16[1,384,2560]{2,1,0:T(8,128)(2,1)}, u32[]{:S(2)}) copy-start(bf16[1,384,2560]{2,1,0:T(8,128)(2,1)} %param.11) | copy-start | bytes 5898244
  31.5 1.2 copy-start.2
  32.6 31.5 %collective-permute-start = (bf16[256,2560]{1,0:T(8,128)(2,1)S(1)}, bf16[256,2560]{1,0:T(8,128)(2,1)S(1)}, u32[]{:S(2)}, u32[]{:S(2)}) collective-permute-start(bf16[256,2560]{1,0:T(8,128)(2,1)S(1)} %bitcast.61), channel_id=1, source_target_pairs={{4,0},{6,2},{8,4},{10,6},{12,8},{14,10},{16,12},{18,14},{20,16},{2... | collective-permute-start | bytes 3932168 | tf_op jit(solution)/shard_map/ppermute | solution.py:16
  64.1 121.0 %copy-start.5 = (bf16[256,2560]{1,0:T(8,128)(2,1)}, bf16[256,2560]{1,0:T(8,128)(2,1)S(1)}, u32[]{:S(2)}) copy-start(bf16[256,2560]{1,0:T(8,128)(2,1)S(1)} %collective-permute-done) | copy-start | bytes 3932164
  64.1 31.5 %collective-permute-start.1 = (bf16[256,2560]{1,0:T(8,128)(2,1)S(1)}, bf16[256,2560]{1,0:T(8,128)(2,1)S(1)}, u32[]{:S(2)}, u32[]{:S(2)}) collective-permute-start(bf16[256,2560]{1,0:T(8,128)(2,1)S(1)} %collective-permute-done), channel_id=1, source_target_pairs={{4,0},{6,2},{8,4},{10,6},{12,8},{14,10},{16,12},{18,14},{20,16},{2... | collective-permute-start | bytes 3932168 | tf_op jit(solution)/shard_map/ppermute | solution.py:16
  95.6 89.5 %copy-start.7 = (bf16[256,2560]{1,0:T(8,128)(2,1)}, bf16[256,2560]{1,0:T(8,128)(2,1)S(1)}, u32[]{:S(2)}) copy-start(bf16[256,2560]{1,0:T(8,128)(2,1)S(1)} %collective-permute-done.1) | copy-start | bytes 3932164
  95.6 30.7 %collective-permute-start.2 = (bf16[256,2560]{1,0:T(8,128)(2,1)S(1)}, bf16[256,2560]{1,0:T(8,128)(2,1)S(1)}, u32[]{:S(2)}, u32[]{:S(2)}) collective-permute-start(bf16[256,2560]{1,0:T(8,128)(2,1)S(1)} %collective-permute-done.1), channel_id=1, source_target_pairs={{4,0},{6,2},{8,4},{10,6},{12,8},{14,10},{16,12},{18,14},{20,16},{2... | collective-permute-start | bytes 3932168 | tf_op jit(solution)/shard_map/ppermute | solution.py:16
  126.3 58.9 %copy-start.9 = (bf16[256,2560]{1,0:T(8,128)(2,1)}, bf16[256,2560]{1,0:T(8,128)(2,1)S(1)}, u32[]{:S(2)}) copy-start(bf16[256,2560]{1,0:T(8,128)(2,1)S(1)} %collective-permute-done.2) | copy-start | bytes 3932164
  126.3 29.8 %collective-permute-start.3 = (bf16[256,2560]{1,0:T(8,128)(2,1)S(1)}, bf16[256,2560]{1,0:T(8,128)(2,1)S(1)}, u32[]{:S(2)}, u32[]{:S(2)}) collective-permute-start(bf16[256,2560]{1,0:T(8,128)(2,1)S(1)} %collective-permute-done.2), channel_id=1, source_target_pairs={{4,0},{6,2},{8,4},{10,6},{12,8},{14,10},{16,12},{18,14},{20,16},{2... | collective-permute-start | bytes 3932168 | tf_op jit(solution)/shard_map/ppermute | solution.py:16
  156.1 29.1 %copy-start.11 = (bf16[256,2560]{1,0:T(8,128)(2,1)}, bf16[256,2560]{1,0:T(8,128)(2,1)S(1)}, u32[]{:S(2)}) copy-start(bf16[256,2560]{1,0:T(8,128)(2,1)S(1)} %collective-permute-done.3) | copy-start | bytes 3932164
  156.1 29.0 %collective-permute-start.4 = (bf16[256,2560]{1,0:T(8,128)(2,1)S(1)}, bf16[256,2560]{1,0:T(8,128)(2,1)}, u32[]{:S(2)}, u32[]{:S(2)}) collective-permute-start(bf16[256,2560]{1,0:T(8,128)(2,1)S(1)} %collective-permute-done.3), channel_id=1, source_target_pairs={{4,0},{6,2},{8,4},{10,6},{12,8},{14,10},{16,12},{18,14},{20,16},{2... | collective-permute-start | bytes 3932168 | tf_op jit(solution)/shard_map/ppermute | solution.py:16
  185.1 29.0 %collective-permute-start.5 = (bf16[256,2560]{1,0:T(8,128)(2,1)}, bf16[256,2560]{1,0:T(8,128)(2,1)}, u32[]{:S(2)}, u32[]{:S(2)}) collective-permute-start(bf16[256,2560]{1,0:T(8,128)(2,1)} %collective-permute-done.4), channel_id=1, source_target_pairs={{4,0},{6,2},{8,4},{10,6},{12,8},{14,10},{16,12},{18,14},{20,16},{2... | collective-permute-start | bytes 3932168 | tf_op jit(solution)/shard_map/ppermute | solution.py:16
  190.0 25.4 %copy-start.13 = (f32[1,8]{1,0:T(1,128)S(1)}, f32[1,8]{1,0:T(1,128)}, u32[]{:S(2)}) copy-start(f32[1,8]{1,0:T(1,128)} %param.13) | copy-start | bytes 100
  190.0 31.5 %copy-start.14 = (bf16[1,2560]{1,0:T(2,128)(2,1)S(1)}, bf16[1,2560]{1,0:T(2,128)(2,1)}, u32[]{:S(2)}) copy-start(bf16[1,2560]{1,0:T(2,128)(2,1)} %param.12) | copy-start | bytes 15364
  191.2 32.3 %all-to-all-start.1 = ((bf16[128,2,2560]{2,0,1:T(8,128)(2,1)}), bf16[128,2,2560]{2,0,1:T(8,128)(2,1)S(1)}, u32[]{:S(2)}, u32[]{:S(2)}) async-start(bf16[128,2,2560]{2,0,1:T(8,128)(2,1)} %copy.14), calls=%async_computation.1 | async-start | bytes 2621440 | tf_op jit(solution)/shard_map/all_to_all | solution.py:32
  194.9 76.4 %reduce-scatter.2.cloned.1.call-start = ((), (), s32[]{:S(2)}) async-start(), calls=%async_computation.3 | async-start | bytes 589824 | tf_op jit(solution)/shard_map/reduce_scatter | solution.py:65
  214.1 27.6 %collective-permute-start.6 = (bf16[256,2560]{1,0:T(8,128)(2,1)}, bf16[256,2560]{1,0:T(8,128)(2,1)}, u32[]{:S(2)}, u32[]{:S(2)}) collective-permute-start(bf16[256,2560]{1,0:T(8,128)(2,1)} %collective-permute-done.5), channel_id=1, source_target_pairs={{4,0},{6,2},{8,4},{10,6},{12,8},{14,10},{16,12},{18,14},{20,16},{2... | collective-permute-start | bytes 3932168 | tf_op jit(solution)/shard_map/ppermute | solution.py:16
  224.2 17.5 %copy-start.3 = (bf16[128,2,2560]{2,0,1:T(8,128)(2,1)S(1)}, bf16[128,2,2560]{2,0,1:T(8,128)(2,1)}, u32[]{:S(2)}) copy-start(bf16[128,2,2560]{2,0,1:T(8,128)(2,1)} %copy-done.2) | copy-start | bytes 3932164
  224.2 17.5 %copy-start.6 = (bf16[256,2560]{1,0:T(8,128)(2,1)S(1)}, bf16[256,2560]{1,0:T(8,128)(2,1)}, u32[]{:S(2)}) copy-start(bf16[256,2560]{1,0:T(8,128)(2,1)} %copy-done.5) | copy-start | bytes 3932164
  224.2 17.5 %copy-start.8 = (bf16[256,2560]{1,0:T(8,128)(2,1)S(1)}, bf16[256,2560]{1,0:T(8,128)(2,1)}, u32[]{:S(2)}) copy-start(bf16[256,2560]{1,0:T(8,128)(2,1)} %copy-done.7) | copy-start | bytes 3932164
  224.2 17.5 %copy-start.10 = (bf16[256,2560]{1,0:T(8,128)(2,1)S(1)}, bf16[256,2560]{1,0:T(8,128)(2,1)}, u32[]{:S(2)}) copy-start(bf16[256,2560]{1,0:T(8,128)(2,1)} %copy-done.9) | copy-start | bytes 3932164
  224.2 17.5 %copy-start.12 = (bf16[256,2560]{1,0:T(8,128)(2,1)S(1)}, bf16[256,2560]{1,0:T(8,128)(2,1)}, u32[]{:S(2)}) copy-start(bf16[256,2560]{1,0:T(8,128)(2,1)} %copy-done.11) | copy-start | bytes 3932164
  272.6 9.3 %copy-start.1 = (f32[256,2560]{1,0:T(8,128)S(1)}, f32[256,2560]{1,0:T(8,128)}, u32[]{:S(2)}) copy-start(f32[256,2560]{1,0:T(8,128)} %bitcast_multiply_fusion) | copy-start | bytes 7864324
  272.6 9.3 %copy-start.4 = (bf16[1,2560,384]{2,1,0:T(8,128)(2,1)S(1)}, bf16[1,2560,384]{2,1,0:T(8,128)(2,1)}, u32[]{:S(2)}) copy-start(bf16[1,2560,384]{2,1,0:T(8,128)(2,1)} %param.10) | copy-start | bytes 5898244
Sparse Core Ops, SparseCore 0:
  256.1 15.0 reduce-scatter.1
where the time goes:
time: 291 us; the launch traced here: 290 us
  waiting for transfers between devices  185 us (64%)
  blocking collectives  36.8 us (13%)
  other arithmetic  16.3 us (6%)
  local copies, waits for them, and re-layouts  16.2 us (6%)
  between operations  14.3 us (5%)
  starting transfers between devices  12.6 us (4%)
  matrix products  9.33 us (3%)
    ppermute x7, waiting for transfers between devices, from_behind(): lax.ppermute(value, axis, [(source, source + steps) for source in range(i...  182 us
    all_to_all x1, blocking collectives, local(): lax.all_to_all(mix_grad[0], 'dp', split_axis=1, concat_axis=0, tiled=True)  20.4 us
    reduce_sum x1, other arithmetic, absorb(): return (grad_sum + weights[member] * values, jnp.sum(values * layer_out))  10.6 us
    ppermute x7, starting transfers between devices, from_behind(): lax.ppermute(value, axis, [(source, source + steps) for source in range(i...  8.97 us
  transfers between devices with their start and end apart: 9, of which 8 were waited for; matrix products, arithmetic and copies ran while one was open for 4% of the time, Pallas kernels for 0%

commit v1 on v0

v1 whole, which is shorter than its diff:
```python
import functools

import jax
import jax.numpy as jnp
from jax import lax
from jax.experimental import pallas as pl
from jax.experimental.pallas import tpu as pltpu
from jax.sharding import PartitionSpec as P

MIXES = 8
LEVELS = MIXES // 2
CHUNK = 32
TILE = 640

epsilon = 1e-06
root_coef = 0.7978845608028654
MESH = pl.DeviceIdType.MESH
F32 = jnp.float32
BF16 = jnp.bfloat16


def gelu_pair(values):
    tangent = jnp.tanh(root_coef * (values + 0.044715 * values * values * values))
    result = 0.5 * values * (1.0 + tangent)
    slopes = 0.5 * (1.0 + tangent) + 0.5 * values * (1.0 - tangent * tangent) * root_coef * (
        1.0 + 3.0 * 0.044715 * values * values
    )
    return (result, slopes)


def fold(values):
    rows, cols = values.shape
    total = jnp.sum(values.reshape(rows // 8, 8, cols), axis=0)
    out = total[:, 0:128]
    for at in range(128, cols, 128):
        out = out + total[:, at : at + 128]
    return out


def kernel(
    n, stride,
    x_ref, lat_ref, g_ref, down_ref, up_ref, gain_ref, wrel_ref,
    upg_ref, dng_ref, gaing_ref, mix_ref,
    xo, cin, latv, gb, inv, actv, slopes, lown, lpeer, sacc, sout, og, mixacc,
    mst, mrecv_y, msx, mrecv_dp, wpeer, upv, downv, apart, apown, rsb, lg,
    loc, gsend, grecv, xsend, xrecv, tsend, trecv, isend, irecv, wsem, zsend, zrecv,
    ssend, srecv, lsend, lrecv, rsend, rrecv, asend, arecv, mysem, msend, mrecv,
):
    own_rows, width = x_ref.shape
    feats = width // n
    half = own_rows // 2
    subs = half // CHUNK
    chunks = n * subs
    tiles = feats // TILE

    sec = lax.axis_index("section")
    x = lax.axis_index("dp")
    q = sec // stride
    res = sec % stride
    a = q // 2
    h = q % 2

    def at(level, side):
        return (2 * level + side) * stride + res

    me_y = sec
    other_y = at(a, 1 - h)
    above = at(a + 1, h)
    below = at(a - 1, h)

    def dev(section, dp):
        return {"section": section, "dp": dp}

    def to(k):
        return lax.rem(x + k, n)

    def source(k):
        return lax.rem(x + n - k, n)

    def remote(src, dst, ssem, rsem, section, dp):
        return pltpu.make_async_remote_copy(
            src_ref=src, dst_ref=dst, send_sem=ssem, recv_sem=rsem,
            device_id=dev(section, dp), device_id_type=MESH,
        )

    def rows(start, size, unit):
        return pl.ds(pl.multiple_of(start, unit), size)

    barrier = pltpu.get_barrier_semaphore()
    for k in range(n):
        for e in range(2):
            if k or e:
                pl.semaphore_signal(
                    barrier, inc=1, device_id=dev(other_y if e else me_y, to(k)), device_id_type=MESH
                )

    @pl.when(a > 0)
    def _():
        pl.semaphore_signal(barrier, inc=1, device_id=dev(below, x), device_id_type=MESH)

    @pl.when(a < LEVELS - 1)
    def _():
        pl.semaphore_signal(barrier, inc=1, device_id=dev(above, x), device_id_type=MESH)

    own_cols = rows(x * feats, feats, 128)
    own_block = rows(x * own_rows, own_rows, own_rows)
    local = [
        pltpu.make_async_copy(
            g_ref.at[rows(h * half, half, half), own_cols], gb.at[h, rows(x * half, half, half)], loc.at[0]
        ),
        pltpu.make_async_copy(lat_ref, latv.at[own_block], loc.at[1]),
        pltpu.make_async_copy(x_ref, xo, loc.at[2]),
        pltpu.make_async_copy(x_ref.at[:, own_cols], cin.at[own_block], loc.at[3]),
        pltpu.make_async_copy(up_ref, upv, loc.at[4]),
        pltpu.make_async_copy(down_ref, downv, loc.at[5]),
    ]
    for copy in local:
        copy.start()

    neighbours = jnp.where(a > 0, 1, 0) + jnp.where(a < LEVELS - 1, 1, 0)
    pl.semaphore_wait(barrier, 2 * n - 1 + neighbours)

    sends = []

    def go(copy):
        copy.start()
        sends.append(copy)
        return copy

    def g_copy(k, e):
        side = 1 - h if e else h
        return remote(
            g_ref.at[rows(side * half, half, half), rows(to(k) * feats, feats, 128)],
            gb.at[h, rows(x * half, half, half)],
            gsend.at[e * n + k], grecv.at[e * n + k],
            other_y if e else me_y, to(k),
        )

    def g_arrival(k, e):
        slot = 1 - h if e else h
        dst = gb.at[slot, rows(source(k) * half, half, half)]
        return remote(dst, dst, gsend.at[e * n + k], grecv.at[e * n + k], me_y, to(k) if k else x)

    go(g_copy(0, 1))
    w_copy = go(remote(wrel_ref, wpeer, wsem.at[0], wsem.at[1], other_y, x))
    for k in range(1, n):
        go(remote(lat_ref, latv.at[own_block], tsend.at[k], trecv.at[k], me_y, to(k)))
        go(g_copy(k, 0))
        go(g_copy(k, 1))
    for k in range(1, n):
        go(remote(
            x_ref.at[:, rows(to(k) * feats, feats, 128)], cin.at[own_block],
            xsend.at[k], xrecv.at[k], me_y, to(k),
        ))

    def arrival(dst, ssem, rsem):
        return remote(dst, dst, ssem, rsem, other_y, x)

    def chunk_at(c):
        k, sub = divmod(c, subs)
        return source(k), k, sub

    def z_copy(slot, c):
        j, _, sub = chunk_at(c)
        span = rows(j * half + sub * CHUNK, CHUNK, CHUNK)
        return remote(
            gb.at[slot, span], gb.at[slot + 2, span], zsend.at[slot, c], zrecv.at[slot + 2, c], below, x
        )

    def z_arrival(slot, c):
        j, _, sub = chunk_at(c)
        dst = gb.at[slot, rows(j * half + sub * CHUNK, CHUNK, CHUNK)]
        return remote(dst, dst, zsend.at[slot - 2, c], zrecv.at[slot, c], other_y, x)

    def flow(c):
        j, k, sub = chunk_at(c)
        if sub == 0:
            if k == 0:
                local[0].wait()
            else:
                g_arrival(k, 0).wait_recv()
            g_arrival(k, 1).wait_recv()

        @pl.when(a > 0)
        def _():
            z_copy(0, c).start()
            z_copy(1, c).start()

        for d in range(1, LEVELS):
            @pl.when(a + d < LEVELS)
            def _():
                for slot in (2 * d, 2 * d + 1):
                    z_arrival(slot, c).wait_recv()
                    if d < LEVELS - 1:
                        @pl.when(a > 0)
                        def _():
                            z_copy(slot, c).start()

    def weight(ref, slot):
        return ref[slot : slot + 1, 0:1]

    def combine(c):
        j, _, sub = chunk_at(c)
        span = rows(j * half + sub * CHUNK, CHUNK, CHUNK)
        for d in range(LEVELS):
            @pl.when(a + d < LEVELS)
            def _():
                @pl.loop(0, tiles)
                def _(t):
                    cols = rows(t * TILE, TILE, 128)
                    first = gb[2 * d, span, cols].astype(F32)
                    second = gb[2 * d + 1, span, cols].astype(F32)
                    for bb, ref in ((0, wrel_ref), (1, wpeer)):
                        value = weight(ref, 2 * d) * first + weight(ref, 2 * d + 1) * second
                        if d:
                            value = sacc[bb, :, cols] + value
                        sacc[bb, :, cols] = value

        @pl.loop(0, tiles)
        def _(t):
            cols = rows(t * TILE, TILE, 128)
            og[rows(j * own_rows + h * half + sub * CHUNK, CHUNK, CHUNK), cols] = sacc[0, :, cols].astype(BF16)
            sout[span, cols] = sacc[1, :, cols].astype(BF16)

        go(remote(
            sout.at[span], og.at[rows(j * own_rows + h * half + sub * CHUNK, CHUNK, CHUNK)],
            ssend.at[c], srecv.at[c], other_y, x,
        ))

    def s_arrival(c):
        j, _, sub = chunk_at(c)
        return arrival(
            og.at[rows(j * own_rows + (1 - h) * half + sub * CHUNK, CHUNK, CHUNK)], ssend.at[c], srecv.at[c]
        )

    def inner(c):
        j, k, sub = chunk_at(c)
        span = rows(j * half + sub * CHUNK, CHUNK, CHUNK)
        own_span = rows(j * own_rows + h * half + sub * CHUNK, CHUNK, CHUNK)
        if sub == 0:
            arrival(lpeer.at[rows(j * half, half, half)], lsend.at[k], lrecv.at[k]).wait_recv()
        for d in range(LEVELS):
            @pl.when(a + d < LEVELS)
            def _():
                @pl.loop(0, tiles)
                def _(t):
                    cols = rows(t * TILE, TILE, 128)
                    mine = lown[own_span, cols].astype(F32)
                    theirs = lpeer[span, cols].astype(F32)
                    for slot in (2 * d, 2 * d + 1):
                        values = gb[slot, span, cols].astype(F32)
                        mixacc[slot] += fold(values * mine)
                        mixacc[8 + slot] += fold(values * theirs)

    mixacc[...] = jnp.zeros_like(mixacc)
    local[2].wait()

    def square(t, total):
        part = xo[:, rows(t * TILE, TILE, 128)].astype(F32)
        part = part * part
        for at_col in range(0, TILE, 128):
            total = total + part[:, at_col : at_col + 128]
        return total

    lanes = lax.fori_loop(0, width // TILE, square, jnp.zeros((own_rows, 128), F32))
    mean_sq = jnp.sum(lanes, axis=1, keepdims=True) / width
    inv[own_block] = jnp.broadcast_to(lax.rsqrt(mean_sq + epsilon), (own_rows, 128))
    for k in range(1, n):
        go(remote(inv.at[own_block], inv.at[own_block], isend.at[k], irecv.at[k], me_y, to(k)))

    arrival(wpeer, wsem.at[0], wsem.at[1]).wait_recv()
    flow(0)

    local[1].wait()
    for k in range(1, n):
        arrival(latv.at[rows(source(k) * own_rows, own_rows, own_rows)], tsend.at[k], trecv.at[k]).wait_recv()
    _, own_slopes = gelu_pair(latv[own_block].astype(F32))
    slopes[...] = own_slopes
    for j in range(n):
        block = slice(j * own_rows, (j + 1) * own_rows)
        values, _ = gelu_pair(latv[block].astype(F32))
        actv[block] = values.astype(BF16)
    local[4].wait()
    local[3].wait()

    def layer_out(k):
        j = source(k)
        block = rows(j * own_rows, own_rows, own_rows)
        if k:
            arrival(cin.at[block], xsend.at[k], xrecv.at[k]).wait_recv()

        @pl.loop(0, tiles)
        def _(t):
            cols = rows(t * TILE, TILE, 128)
            branch = jnp.dot(actv[block, :], upv[:, cols], preferred_element_type=F32)
            lown[block, cols] = (cin[block, cols].astype(F32) + branch).astype(BF16)

        go(remote(
            lown.at[rows(j * own_rows + (1 - h) * half, half, half)], lpeer.at[rows(j * half, half, half)],
            lsend.at[k], lrecv.at[k], other_y, x,
        ))

    def act_block(k):
        j = source(k)
        for sub in range(subs):
            s_arrival(k * subs + sub).wait_recv()
        part = lax.dot_general(
            og[rows(j * own_rows, own_rows, own_rows), :], upv[...], (((1,), (1,)), ((), ())),
            preferred_element_type=F32,
        )
        if k == 0:
            apown[...] = part
        else:
            apart[k] = part.astype(BF16)
            go(remote(apart.at[k], rsb.at[k], rsend.at[k], rrecv.at[k], me_y, j))

    layer_out(0)
    combine(0)
    for c in range(1, chunks):
        k, sub = divmod(c, subs)
        flow(c)
        combine(c)
        inner(c - 1)
        if sub == 0:
            layer_out(k)
            act_block(k - 1)
    act_block(n - 1)
    inner(chunks - 1)

    for bb in range(2):
        for slot in range(8):
            mst[bb, slot : slot + 1] = jnp.sum(mixacc[8 * bb + slot], axis=0, keepdims=True)
    go(remote(mst.at[1], mrecv_y, mysem.at[0], mysem.at[1], other_y, x))

    total = apown[...]
    for k in range(1, n):
        arrival(rsb.at[k], rsend.at[k], rrecv.at[k]).wait_recv()
        total = total + rsb[k].astype(F32)
    lg[own_block] = (total * slopes[...]).astype(BF16)
    for k in range(1, n):
        go(remote(lg.at[own_block], lg.at[own_block], asend.at[k], arecv.at[k], me_y, to(k)))

    arrival(mrecv_y, mysem.at[0], mysem.at[1]).wait_recv()
    msx[...] = mst[0] + mrecv_y[...]
    for k in range(1, n):
        go(remote(msx, mrecv_dp.at[k], msend.at[k], mrecv.at[k], me_y, to(k)))

    @pl.loop(0, tiles)
    def _(t):
        cols = rows(t * TILE, TILE, 128)
        upg_ref[:, cols] = lax.dot_general(
            actv[...], og[:, cols], (((0,), (0,)), ((), ())), preferred_element_type=F32
        ).astype(BF16)

    mixed = msx[...]
    for k in range(1, n):
        arrival(mrecv_dp.at[k], msend.at[k], mrecv.at[k]).wait_recv()
        mixed = mixed + mrecv_dp[k]
    mix_ref[...] = mixed

    for k in range(1, n):
        block = rows(source(k) * own_rows, own_rows, own_rows)
        arrival(inv.at[block], isend.at[k], irecv.at[k]).wait_recv()
        arrival(lg.at[block], asend.at[k], arecv.at[k]).wait_recv()
    local[5].wait()

    @pl.loop(0, tiles)
    def _(t):
        cols = rows(t * TILE, TILE, 128)
        scaled = cin[:, cols].astype(F32) * inv[:, 0:1]
        normed = (scaled * gain_ref[:, cols].astype(F32)).astype(BF16)
        dng_ref[rows(t * TILE, TILE, 128), :] = lax.dot_general(
            normed, lg[...], (((0,), (0,)), ((), ())), preferred_element_type=F32
        ).astype(BF16)
        norm_grad = lax.dot_general(
            lg[...], downv[rows(t * TILE, TILE, 128), :], (((1,), (1,)), ((), ())),
            preferred_element_type=F32,
        )
        gaing_ref[:, cols] = jnp.sum(norm_grad * scaled, axis=0, keepdims=True)

    for copy in sends:
        copy.wait_send()

    @pl.when(a > 0)
    def _():
        for c in range(chunks):
            z_copy(0, c).wait_send()
            z_copy(1, c).wait_send()
        for d in range(1, LEVELS - 1):
            @pl.when(a + d < LEVELS)
            def _():
                for c in range(chunks):
                    z_copy(2 * d, c).wait_send()
                    z_copy(2 * d + 1, c).wait_send()


def local(layer_in, latent, mix_grad, down_proj, up_proj, norm_gain, mix_weight):
    _, own_rows, width = layer_in.shape
    n = lax.axis_size("dp")
    stride = lax.axis_size("section") // MIXES
    latents = latent.shape[2]
    feats = width // n
    tokens = own_rows * n
    chunks = tokens // 2 // CHUNK
    side = (lax.axis_index("section") // stride) % 2
    row = mix_weight[0]
    zero = jnp.zeros((1,), F32)
    rel = jnp.where(side == 1, jnp.concatenate([zero, row[:-1]]), row)
    rel = jnp.broadcast_to(rel[:, None], (MIXES, 128))
    dma = pltpu.SemaphoreType.DMA
    anyspace = pl.BlockSpec(memory_space=pl.ANY)
    vmem = pl.BlockSpec(memory_space=pltpu.VMEM)
    up_grad, down_grad, gain_grad, mixed = pl.pallas_call(
        functools.partial(kernel, n, stride),
        out_shape=(
            jax.ShapeDtypeStruct((latents, feats), BF16),
            jax.ShapeDtypeStruct((feats, latents), BF16),
            jax.ShapeDtypeStruct((1, feats), F32),
            jax.ShapeDtypeStruct((MIXES, 128), F32),
        ),
        in_specs=[anyspace] * 5 + [vmem] * 2,
        out_specs=(vmem,) * 4,
        scratch_shapes=[
            pltpu.VMEM((own_rows, width), BF16),
            pltpu.VMEM((tokens, feats), BF16),
            pltpu.VMEM((tokens, latents), BF16),
            pltpu.VMEM((MIXES, tokens // 2, feats), BF16),
            pltpu.VMEM((tokens, 128), F32),
            pltpu.VMEM((tokens, latents), BF16),
            pltpu.VMEM((own_rows, latents), F32),
            pltpu.VMEM((tokens, feats), BF16),
            pltpu.VMEM((tokens // 2, feats), BF16),
            pltpu.VMEM((2, CHUNK, feats), F32),
            pltpu.VMEM((tokens // 2, feats), BF16),
            pltpu.VMEM((tokens, feats), BF16),
            pltpu.VMEM((16, 8, 128), F32),
            pltpu.VMEM((2, 8, 128), F32),
            pltpu.VMEM((8, 128), F32),
            pltpu.VMEM((8, 128), F32),
            pltpu.VMEM((n, 8, 128), F32),
            pltpu.VMEM((8, 128), F32),
            pltpu.VMEM((latents, feats), BF16),
            pltpu.VMEM((feats, latents), BF16),
            pltpu.VMEM((n, own_rows, latents), BF16),
            pltpu.VMEM((own_rows, latents), F32),
            pltpu.VMEM((n, own_rows, latents), BF16),
            pltpu.VMEM((tokens, latents), BF16),
            dma((6,)),
            dma((2 * n,)), dma((2 * n,)),
            dma((n,)), dma((n,)),
            dma((n,)), dma((n,)),
            dma((n,)), dma((n,)),
            dma((2,)),
            dma((MIXES, chunks)), dma((MIXES, chunks)),
            dma((chunks,)), dma((chunks,)),
            dma((n,)), dma((n,)),
            dma((n,)), dma((n,)),
            dma((n,)), dma((n,)),
            dma((2,)),
            dma((n,)), dma((n,)),
        ],
        compiler_params=pltpu.CompilerParams(
            collective_id=0, has_side_effects=True, vmem_limit_bytes=60 * 1024 * 1024
        ),
    )(layer_in[0], latent[0], mix_grad[0], down_proj[0], up_proj[0], norm_gain, rel)
    sums = jnp.sum(mixed, axis=1)
    mixing = jnp.where(side == 1, jnp.concatenate([sums[1:], zero]), sums)
    return (up_grad[None], down_grad[None], gain_grad, mixing[None])


def solution(mesh):
    return jax.shard_map(
        local,
        mesh=mesh,
        in_specs=(
            P("section", "dp", None),
            P("section", "dp", None),
            P("section", "dp", None),
            P("section", "dp", None),
            P("section", None, "dp"),
            P("section", "dp"),
            P("section", None),
        ),
        out_specs=(
            P("section", None, "dp"),
            P("section", "dp", None),
            P("section", "dp"),
            P("section", None),
        ),
        check_vma=False,
    )
```

time: 291 us -> 128 us (0.44)
  waiting for transfers between devices: 185 us -> 0 us
  Pallas kernels: 0 us -> 118 us
  blocking collectives: 36.8 us -> 0 us
  other arithmetic: 16.3 us -> 2.12 us
  between operations: 14.3 us -> 0.67 us
  starting transfers between devices: 12.6 us -> 0 us
  local copies, waits for them, and re-layouts: 16.2 us -> 6.36 us
  matrix products: 9.33 us -> 0 us
    ppermute x7 -> x0, waiting for transfers between devices: 182 us -> none  [from_behind(): lax.ppermute(value, axis, [(source, source + steps) for source in range(i...]
    pallas_call x0 -> x1, Pallas kernels: none -> 118 us  [local(): pl.pallas_call(functools.partial(kernel, n, stride), out_shape=(jax.Shape...]
    all_to_all x1 -> x0, blocking collectives: 20.4 us -> none  [local(): lax.all_to_all(mix_grad[0], 'dp', split_axis=1, concat_axis=0, tiled=True)]
    all_gather x2 -> x0, blocking collectives: 10.9 us -> none  [the longest x1 5.48 us: local(): latent_all = lax.all_gather(latent[0], 'dp', axis=0, tiled=True)]
    reduce_sum x2 -> x1, other arithmetic: 11 us -> 0.8 us  [local(): sums = jnp.sum(mixed, axis=1)]
    dot_general x5 -> x0, matrix products: 9.33 us -> none  [the longest x1 3.91 us: local(): jnp.einsum('tc,tr->cr', normed, latent_grad, preferred_element_type=jnp.f...]
    ppermute x7 -> x0, starting transfers between devices: 8.97 us -> none  [from_behind(): lax.ppermute(value, axis, [(source, source + steps) for source in range(i...]
    all_to_all x4 -> x0, local copies, waits for them, and re-layouts: 8.61 us -> none  [the longest x2 4.76 us: local(): lax.all_to_all(layer_in[0], 'dp', split_axis=1, concat_axis=0, tiled=True)]
  transfers between devices with their start and end apart: 9 -> 0, of which waited for: 8 -> 0; matrix products, arithmetic and copies ran while one was open for 4% -> 0% of each run, Pallas kernels for 0% -> 0%
where the time goes in v1:
time: 128 us
  Pallas kernels  118 us (92%)
  local copies, waits for them, and re-layouts  6.36 us (5%)
  other arithmetic  2.12 us (2%)
    pallas_call x1, Pallas kernels, local(): pl.pallas_call(functools.partial(kernel, n, stride), out_shape=(jax.Shape...  118 us
    unnamed x7, local copies, waits for them, and re-layouts  4.96 us

profile of v1, /device:TPU:0, one launch (start us, length us, event | category | flops | bytes accessed | tf_op | source)
XLA Modules:
  0.0 127.6 jit_solution(17241586754773440314)
XLA Ops:
  0.7 0.7 slice_bitcast_fusion.1
  1.3 0.7 broadcast_select_fusion.1
  2.1 0.7 broadcast_in_dim.6.wrel_ref
  2.7 118.5 %shard_map.102 = (bf16[384,2560]{1,0:T(8,128)(2,1)}, bf16[2560,384]{1,0:T(8,128)(2,1)}, f32[1,2560]{1,0:T(1,128)}, f32[8,128]{1,0:T(8,128)}) custom-call(bf16[128,5120]{1,0:T(8,128)(2,1)} %bitcast.19, bf16[128,384]{1,0:T(8,128)(2,1)} %bitcast.21, bf16[128,5120]{1,0:T(8,128)(2,1)} %bitcast.20, bf16[2560,384]{1,0:T(8,128)(2,1)} %bitcast.17, ...), custom_call_target="tpu_custom_call" | custom-call | tf_op jit(solution)/shard_map/pallas_call | solution.py:413
  121.2 0.8 reduce_sum.11
  122.0 0.1 slice_bitcast_fusion
  122.1 0.6 broadcast_select_fusion
  122.6 0.0 copy-start
  122.7 3.1 %copy.14 = bf16[1,384,2560]{2,1,0:T(8,128)(2,1)} copy(bf16[1,384,2560]{2,1,0:T(8,128)(2,1)} %bitcast.16) | data formatting | bytes 3932160
  125.7 0.0 copy-done
  125.7 0.0 copy-start.1
  125.7 1.3 copy.15
  127.0 0.0 copy-done.1
  127.0 0.6 copy.16
Async XLA Ops:
  122.6 3.1 %copy-start = (bf16[2560,384]{1,0:T(8,128)(2,1)S(1)}, bf16[2560,384]{1,0:T(8,128)(2,1)}, u32[]{:S(2)}) copy-start(bf16[2560,384]{1,0:T(8,128)(2,1)} %get-tuple-element.9) | copy-start | bytes 5898244
  125.7 1.3 %copy-start.1 = (f32[1,2560]{1,0:T(1,128)S(1)}, f32[1,2560]{1,0:T(1,128)}, u32[]{:S(2)}) copy-start(f32[1,2560]{1,0:T(1,128)} %get-tuple-element.18) | copy-start | bytes 30724

commit v2 on v1

--- a/solution.py
+++ b/solution.py
@@ -9,7 +9,9 @@
 
 MIXES = 8
 LEVELS = MIXES // 2
-CHUNK = 32
+REACH = LEVELS - 1
+SLOTS = 2 * REACH
+CHUNK = 16
 TILE = 640
 
 epsilon = 1e-06
@@ -43,7 +45,9 @@
     upg_ref, dng_ref, gaing_ref, mix_ref,
     xo, cin, latv, gb, inv, actv, slopes, lown, lpeer, sacc, sout, og, mixacc,
     mst, mrecv_y, msx, mrecv_dp, wpeer, upv, downv, apart, apown, rsb, lg,
+    wlow, llow, lowacc, s0out, s0in, mixlow, mlow, mlowin,
     loc, gsend, grecv, xsend, xrecv, tsend, trecv, isend, irecv, wsem, zsend, zrecv,
+    wlsend, wlrecv, llsend, llrecv, s0send, s0recv, mlsend, mlrecv,
     ssend, srecv, lsend, lrecv, rsend, rrecv, asend, arecv, mysem, msend, mrecv,
 ):
     own_rows, width = x_ref.shape
@@ -172,6 +176,9 @@
         dst = gb.at[slot, rows(j * half + sub * CHUNK, CHUNK, CHUNK)]
         return remote(dst, dst, zsend.at[slot - 2, c], zrecv.at[slot, c], other_y, x)
 
+    def holds(d):
+        return (a + d < LEVELS) if d == 0 else jnp.logical_and(a > 0, a + d < LEVELS)
+
     def flow(c):
         j, k, sub = chunk_at(c)
         if sub == 0:
@@ -181,29 +188,79 @@
                 g_arrival(k, 0).wait_recv()
             g_arrival(k, 1).wait_recv()
 
-        @pl.when(a > 0)
+        @pl.when(a > 1)
         def _():
             z_copy(0, c).start()
             z_copy(1, c).start()
 
-        for d in range(1, LEVELS):
-            @pl.when(a + d < LEVELS)
+        for d in range(1, REACH):
+            @pl.when(holds(d))
             def _():
                 for slot in (2 * d, 2 * d + 1):
                     z_arrival(slot, c).wait_recv()
-                    if d < LEVELS - 1:
-                        @pl.when(a > 0)
+                    if d < REACH - 1:
+                        @pl.when(a > 1)
                         def _():
                             z_copy(slot, c).start()
 
     def weight(ref, slot):
         return ref[slot : slot + 1, 0:1]
+
+    def s0_copy(bb, c):
+        j, _, sub = chunk_at(c)
+        span = rows(j * half + sub * CHUNK, CHUNK, CHUNK)
+        return remote(
+            s0out.at[bb, span], s0in.at[bb, span], s0send.at[bb, c], s0recv.at[bb, c], below, x
+        )
+
+    def low_copy(bb, k):
+        j = source(k)
+        span = rows(j * half, half, half)
+        src = lpeer.at[span] if bb else lown.at[rows(j * own_rows + h * half, half, half)]
+        return remote(src, llow.at[bb, span], llsend.at[bb, k], llrecv.at[bb, k], above, x)
+
+    def wlow_copy(bb):
+        return remote(wpeer if bb else wrel_ref, wlow.at[bb], wlsend.at[bb], wlrecv.at[bb], above, x)
+
+    def mlow_copy():
+        return remote(mlow, mlowin, mlsend.at[0], mlrecv.at[0], below, x)
+
+    def low_inner(c):
+        j, k, sub = chunk_at(c)
+        span = rows(j * half + sub * CHUNK, CHUNK, CHUNK)
+        if sub == 0:
+            for bb in range(2):
+                low_copy(bb, k).wait_recv()
+
+        @pl.loop(0, tiles)
+        def _(t):
+            cols = rows(t * TILE, TILE, 128)
+            mine = llow[0, span, cols].astype(F32)
+            theirs = llow[1, span, cols].astype(F32)
+            for slot in range(SLOTS):
+                values = gb[slot, span, cols].astype(F32)
+                lowacc[slot + 2] += fold(values * mine)
+                lowacc[8 + slot + 2] += fold(values * theirs)
 
     def combine(c):
         j, _, sub = chunk_at(c)
         span = rows(j * half + sub * CHUNK, CHUNK, CHUNK)
-        for d in range(LEVELS):
-            @pl.when(a + d < LEVELS)
+        @pl.when(a == 1)
+        def _():
+            @pl.loop(0, tiles)
+            def _(t):
+                cols = rows(t * TILE, TILE, 128)
+                for bb in range(2):
+                    value = jnp.zeros((CHUNK, TILE), F32)
+                    for slot in range(SLOTS):
+                        value = value + wlow[bb, slot + 2 : slot + 3, 0:1] * gb[slot, span, cols].astype(F32)
+                    s0out[bb, span, cols] = value.astype(BF16)
+
+            for bb in range(2):
+                s0_copy(bb, c).start()
+
+        for d in range(REACH):
+            @pl.when(holds(d))
             def _():
                 @pl.loop(0, tiles)
                 def _(t):
@@ -216,6 +273,17 @@
                             value = sacc[bb, :, cols] + value
                         sacc[bb, :, cols] = value
 
+        @pl.when(a == 0)
+        def _():
+            for bb in range(2):
+                s0_copy(bb, c).wait_recv()
+
+            @pl.loop(0, tiles)
+            def _(t):
+                cols = rows(t * TILE, TILE, 128)
+                for bb in range(2):
+                    sacc[bb, :, cols] += s0in[bb, span, cols].astype(F32)
+
         @pl.loop(0, tiles)
         def _(t):
             cols = rows(t * TILE, TILE, 128)
@@ -239,8 +307,12 @@
         own_span = rows(j * own_rows + h * half + sub * CHUNK, CHUNK, CHUNK)
         if sub == 0:
             arrival(lpeer.at[rows(j * half, half, half)], lsend.at[k], lrecv.at[k]).wait_recv()
-        for d in range(LEVELS):
-            @pl.when(a + d < LEVELS)
+
+            @pl.when(a == 0)
+            def _():
+                low_copy(1, k).start()
+        for d in range(REACH):
+            @pl.when(holds(d))
             def _():
                 @pl.loop(0, tiles)
                 def _(t):
@@ -253,6 +325,7 @@
                         mixacc[8 + slot] += fold(values * theirs)
 
     mixacc[...] = jnp.zeros_like(mixacc)
+    lowacc[...] = jnp.zeros_like(lowacc)
     local[2].wait()
 
     def square(t, total):
@@ -269,6 +342,12 @@
         go(remote(inv.at[own_block], inv.at[own_block], isend.at[k], irecv.at[k], me_y, to(k)))
 
     arrival(wpeer, wsem.at[0], wsem.at[1]).wait_recv()
+
+    @pl.when(a == 0)
+    def _():
+        for bb in range(2):
+            wlow_copy(bb).start()
+
     flow(0)
 
     local[1].wait()
@@ -299,6 +378,10 @@
             lown.at[rows(j * own_rows + (1 - h) * half, half, half)], lpeer.at[rows(j * half, half, half)],
             lsend.at[k], lrecv.at[k], other_y, x,
         ))
+
+        @pl.when(a == 0)
+        def _():
+            low_copy(0, k).start()
 
     def act_block(k):
         j = source(k)
@@ -315,6 +398,12 @@
             go(remote(apart.at[k], rsb.at[k], rsend.at[k], rrecv.at[k], me_y, j))
 
     layer_out(0)
+
+    @pl.when(a == 1)
+    def _():
+        for bb in range(2):
+            wlow_copy(bb).wait_recv()
+
     combine(0)
     for c in range(1, chunks):
         k, sub = divmod(c, subs)
@@ -324,26 +413,8 @@
         if sub == 0:
             layer_out(k)
             act_block(k - 1)
+    inner(chunks - 1)
     act_block(n - 1)
-    inner(chunks - 1)
-
-    for bb in range(2):
-        for slot in range(8):
-            mst[bb, slot : slot + 1] = jnp.sum(mixacc[8 * bb + slot], axis=0, keepdims=True)
-    go(remote(mst.at[1], mrecv_y, mysem.at[0], mysem.at[1], other_y, x))
-
-    total = apown[...]
-    for k in range(1, n):
-        arrival(rsb.at[k], rsend.at[k], rrecv.at[k]).wait_recv()
-        total = total + rsb[k].astype(F32)
-    lg[own_block] = (total * slopes[...]).astype(BF16)
-    for k in range(1, n):
-        go(remote(lg.at[own_block], lg.at[own_block], asend.at[k], arecv.at[k], me_y, to(k)))
-
-    arrival(mrecv_y, mysem.at[0], mysem.at[1]).wait_recv()
-    msx[...] = mst[0] + mrecv_y[...]
-    for k in range(1, n):
-        go(remote(msx, mrecv_dp.at[k], msend.at[k], mrecv.at[k], me_y, to(k)))
 
     @pl.loop(0, tiles)
     def _(t):
@@ -351,6 +422,42 @@
         upg_ref[:, cols] = lax.dot_general(
             actv[...], og[:, cols], (((0,), (0,)), ((), ())), preferred_element_type=F32
         ).astype(BF16)
+
+
+    total = apown[...]
+    for k in range(1, n):
+        arrival(rsb.at[k], rsend.at[k], rrecv.at[k]).wait_recv()
+        total = total + rsb[k].astype(F32)
+    lg[own_block] = (total * slopes[...]).astype(BF16)
+    for k in range(1, n):
+        go(remote(lg.at[own_block], lg.at[own_block], asend.at[k], arecv.at[k], me_y, to(k)))
+
+    @pl.when(a == 1)
+    def _():
+        for c in range(chunks):
+            low_inner(c)
+        for bb in range(2):
+            for slot in range(8):
+                mlow[bb, slot : slot + 1] = jnp.sum(lowacc[8 * bb + slot], axis=0, keepdims=True)
+        mlow_copy().start()
+
+    for bb in range(2):
+        for slot in range(8):
+            mst[bb, slot : slot + 1] = jnp.sum(mixacc[8 * bb + slot], axis=0, keepdims=True)
+
+    mixlow[...] = jnp.zeros_like(mixlow)
+
+    @pl.when(a == 0)
+    def _():
+        mlow_copy().wait_recv()
+        mixlow[...] = mlowin[...]
+
+    mst[...] = mst[...] + mixlow[...]
+    go(remote(mst.at[1], mrecv_y, mysem.at[0], mysem.at[1], other_y, x))
+    arrival(mrecv_y, mysem.at[0], mysem.at[1]).wait_recv()
+    msx[...] = mst[0] + mrecv_y[...]
+    for k in range(1, n):
+        go(remote(msx, mrecv_dp.at[k], msend.at[k], mrecv.at[k], me_y, to(k)))
 
     mixed = msx[...]
     for k in range(1, n):
@@ -381,17 +488,32 @@
     for copy in sends:
         copy.wait_send()
 
-    @pl.when(a > 0)
+    @pl.when(a > 1)
     def _():
         for c in range(chunks):
             z_copy(0, c).wait_send()
             z_copy(1, c).wait_send()
-        for d in range(1, LEVELS - 1):
-            @pl.when(a + d < LEVELS)
-            def _():
-                for c in range(chunks):
-                    z_copy(2 * d, c).wait_send()
-                    z_copy(2 * d + 1, c).wait_send()
+
+    for d in range(1, REACH - 1):
+        @pl.when(jnp.logical_and(a > 1, a + d < LEVELS))
+        def _():
+            for c in range(chunks):
+                z_copy(2 * d, c).wait_send()
+                z_copy(2 * d + 1, c).wait_send()
+
+    @pl.when(a == 1)
+    def _():
+        mlow_copy().wait_send()
+        for c in range(chunks):
+            for bb in range(2):
+                s0_copy(bb, c).wait_send()
+
+    @pl.when(a == 0)
+    def _():
+        for bb in range(2):
+            wlow_copy(bb).wait_send()
+            for k in range(n):
+                low_copy(bb, k).wait_send()
 
 
 def local(layer_in, latent, mix_grad, down_proj, up_proj, norm_gain, mix_weight):
@@ -424,7 +546,7 @@
             pltpu.VMEM((own_rows, width), BF16),
             pltpu.VMEM((tokens, feats), BF16),
             pltpu.VMEM((tokens, latents), BF16),
-            pltpu.VMEM((MIXES, tokens // 2, feats), BF16),
+            pltpu.VMEM((SLOTS, tokens // 2, feats), BF16),
             pltpu.VMEM((tokens, 128), F32),
             pltpu.VMEM((tokens, latents), BF16),
             pltpu.VMEM((own_rows, latents), F32),
@@ -445,13 +567,25 @@
             pltpu.VMEM((own_rows, latents), F32),
             pltpu.VMEM((n, own_rows, latents), BF16),
             pltpu.VMEM((tokens, latents), BF16),
+            pltpu.VMEM((2, 8, 128), F32),
+            pltpu.VMEM((2, tokens // 2, feats), BF16),
+            pltpu.VMEM((16, 8, 128), F32),
+            pltpu.VMEM((2, tokens // 2, feats), BF16),
+            pltpu.VMEM((2, tokens // 2, feats), BF16),
+            pltpu.VMEM((2, 8, 128), F32),
+            pltpu.VMEM((2, 8, 128), F32),
+            pltpu.VMEM((2, 8, 128), F32),
             dma((6,)),
             dma((2 * n,)), dma((2 * n,)),
             dma((n,)), dma((n,)),
             dma((n,)), dma((n,)),
             dma((n,)), dma((n,)),
             dma((2,)),
-            dma((MIXES, chunks)), dma((MIXES, chunks)),
+            dma((SLOTS, chunks)), dma((SLOTS, chunks)),
+            dma((2,)), dma((2,)),
+            dma((2, n)), dma((2, n)),
+            dma((2, chunks)), dma((2, chunks)),
+            dma((1,)), dma((1,)),
             dma((chunks,)), dma((chunks,)),
             dma((n,)), dma((n,)),
             dma((n,)), dma((n,)),

time: 128 us -> 110 us (0.86)
  Pallas kernels: 118 us -> 100 us
    pallas_call x1, Pallas kernels: 118 us -> 100 us  [local(): pl.pallas_call(functools.partial(kernel, n, stride), out_shape=(jax.Shape...]
where the time goes in v2:
time: 110 us; the launch traced here: 109 us
  Pallas kernels  100 us (91%)
  local copies, waits for them, and re-layouts  6.36 us (6%)
  other arithmetic  2.12 us (2%)
    pallas_call x1, Pallas kernels, local(): pl.pallas_call(functools.partial(kernel, n, stride), out_shape=(jax.Shape...  100 us
    unnamed x7, local copies, waits for them, and re-layouts  4.96 us

profile of v2, /device:TPU:0, one launch (start us, length us, event | category | flops | bytes accessed | tf_op | source)
XLA Modules:
  0.0 109.3 jit_solution(11338079059040487105)
XLA Ops:
  0.7 0.7 slice_bitcast_fusion.1
  1.3 0.7 broadcast_select_fusion.1
  2.1 0.7 broadcast_in_dim.6.wrel_ref
  2.7 100.1 %shard_map.102 = (bf16[384,2560]{1,0:T(8,128)(2,1)}, bf16[2560,384]{1,0:T(8,128)(2,1)}, f32[1,2560]{1,0:T(1,128)}, f32[8,128]{1,0:T(8,128)}) custom-call(bf16[128,5120]{1,0:T(8,128)(2,1)} %bitcast.19, bf16[128,384]{1,0:T(8,128)(2,1)} %bitcast.21, bf16[128,5120]{1,0:T(8,128)(2,1)} %bitcast.20, bf16[2560,384]{1,0:T(8,128)(2,1)} %bitcast.17, ...), custom_call_target="tpu_custom_call" | custom-call | tf_op jit(solution)/shard_map/pallas_call | solution.py:535
  102.8 0.8 reduce_sum.11
  103.6 0.1 slice_bitcast_fusion
  103.7 0.6 broadcast_select_fusion
  104.3 0.0 copy-start
  104.3 3.1 %copy.14 = bf16[1,384,2560]{2,1,0:T(8,128)(2,1)} copy(bf16[1,384,2560]{2,1,0:T(8,128)(2,1)} %bitcast.16) | data formatting | bytes 3932160
  107.4 0.0 copy-done
  107.4 0.0 copy-start.1
  107.4 1.3 %copy.15 = bf16[1,2560,384]{2,1,0:T(8,128)(2,1)} copy(bf16[1,2560,384]{2,1,0:T(8,128)(2,1)S(1)} %bitcast.15) | data formatting | bytes 3932160
  108.7 0.0 copy-done.1
  108.7 0.6 copy.16
Async XLA Ops:
  104.3 3.1 %copy-start = (bf16[2560,384]{1,0:T(8,128)(2,1)S(1)}, bf16[2560,384]{1,0:T(8,128)(2,1)}, u32[]{:S(2)}) copy-start(bf16[2560,384]{1,0:T(8,128)(2,1)} %get-tuple-element.9) | copy-start | bytes 5898244
  107.4 1.3 %copy-start.1 = (f32[1,2560]{1,0:T(1,128)S(1)}, f32[1,2560]{1,0:T(1,128)}, u32[]{:S(2)}) copy-start(f32[1,2560]{1,0:T(1,128)} %get-tuple-element.18) | copy-start | bytes 30724

commit v3 on v2

--- a/solution.py
+++ b/solution.py
@@ -41,11 +41,11 @@
 
 def kernel(
     n, stride,
-    x_ref, lat_ref, g_ref, down_ref, up_ref, gain_ref, wrel_ref,
+    x_ref, lat_ref, g_ref, down_ref, up_ref, gain_ref, mw_ref,
     upg_ref, dng_ref, gaing_ref, mix_ref,
     xo, cin, latv, gb, inv, actv, slopes, lown, lpeer, sacc, sout, og, mixacc,
     mst, mrecv_y, msx, mrecv_dp, wpeer, upv, downv, apart, apown, rsb, lg,
-    wlow, llow, lowacc, s0out, s0in, mixlow, mlow, mlowin,
+    wown, wlow, llow, lowacc, s0out, s0in, mixlow, mlow, mlowin,
     loc, gsend, grecv, xsend, xrecv, tsend, trecv, isend, irecv, wsem, zsend, zrecv,
     wlsend, wlrecv, llsend, llrecv, s0send, s0recv, mlsend, mlrecv,
     ssend, srecv, lsend, lrecv, rsend, rrecv, asend, arecv, mysem, msend, mrecv,
@@ -105,6 +105,17 @@
     @pl.when(a < LEVELS - 1)
     def _():
         pl.semaphore_signal(barrier, inc=1, device_id=dev(above, x), device_id_type=MESH)
+
+    @pl.when(h == 0)
+    def _():
+        for slot in range(MIXES):
+            wown[slot : slot + 1] = jnp.broadcast_to(mw_ref[0:1, slot : slot + 1], (1, 128))
+
+    @pl.when(h == 1)
+    def _():
+        wown[0:1] = jnp.zeros((1, 128), F32)
+        for slot in range(1, MIXES):
+            wown[slot : slot + 1] = jnp.broadcast_to(mw_ref[0:1, slot - 1 : slot], (1, 128))
 
     own_cols = rows(x * feats, feats, 128)
     own_block = rows(x * own_rows, own_rows, own_rows)
@@ -146,7 +157,7 @@
         return remote(dst, dst, gsend.at[e * n + k], grecv.at[e * n + k], me_y, to(k) if k else x)
 
     go(g_copy(0, 1))
-    w_copy = go(remote(wrel_ref, wpeer, wsem.at[0], wsem.at[1], other_y, x))
+    w_copy = go(remote(wown, wpeer, wsem.at[0], wsem.at[1], other_y, x))
     for k in range(1, n):
         go(remote(lat_ref, latv.at[own_block], tsend.at[k], trecv.at[k], me_y, to(k)))
         go(g_copy(k, 0))
@@ -220,7 +231,7 @@
         return remote(src, llow.at[bb, span], llsend.at[bb, k], llrecv.at[bb, k], above, x)
 
     def wlow_copy(bb):
-        return remote(wpeer if bb else wrel_ref, wlow.at[bb], wlsend.at[bb], wlrecv.at[bb], above, x)
+        return remote(wpeer if bb else wown, wlow.at[bb], wlsend.at[bb], wlrecv.at[bb], above, x)
 
     def mlow_copy():
         return remote(mlow, mlowin, mlsend.at[0], mlrecv.at[0], below, x)
@@ -267,7 +278,7 @@
                     cols = rows(t * TILE, TILE, 128)
                     first = gb[2 * d, span, cols].astype(F32)
                     second = gb[2 * d + 1, span, cols].astype(F32)
-                    for bb, ref in ((0, wrel_ref), (1, wpeer)):
+                    for bb, ref in ((0, wown), (1, wpeer)):
                         value = weight(ref, 2 * d) * first + weight(ref, 2 * d + 1) * second
                         if d:
                             value = sacc[bb, :, cols] + value
@@ -413,8 +424,25 @@
         if sub == 0:
             layer_out(k)
             act_block(k - 1)
+        if c >= subs:
+            @pl.when(a == 1)
+            def _():
+                low_inner(c - subs)
     inner(chunks - 1)
     act_block(n - 1)
+
+    @pl.when(a == 1)
+    def _():
+        for c in range(chunks - subs, chunks):
+            low_inner(c)
+        for bb in range(2):
+            for slot in range(8):
+                mlow[bb, slot : slot + 1] = jnp.sum(lowacc[8 * bb + slot], axis=0, keepdims=True)
+        mlow_copy().start()
+
+    for bb in range(2):
+        for slot in range(8):
+            mst[bb, slot : slot + 1] = jnp.sum(mixacc[8 * bb + slot], axis=0, keepdims=True)
 
     @pl.loop(0, tiles)
     def _(t):
@@ -432,19 +460,6 @@
     for k in range(1, n):
         go(remote(lg.at[own_block], lg.at[own_block], asend.at[k], arecv.at[k], me_y, to(k)))
 
-    @pl.when(a == 1)
-    def _():
-        for c in range(chunks):
-            low_inner(c)
-        for bb in range(2):
-            for slot in range(8):
-                mlow[bb, slot : slot + 1] = jnp.sum(lowacc[8 * bb + slot], axis=0, keepdims=True)
-        mlow_copy().start()
-
-    for bb in range(2):
-        for slot in range(8):
-            mst[bb, slot : slot + 1] = jnp.sum(mixacc[8 * bb + slot], axis=0, keepdims=True)
-
     mixlow[...] = jnp.zeros_like(mixlow)
 
     @pl.when(a == 0)
@@ -454,22 +469,16 @@
 
     mst[...] = mst[...] + mixlow[...]
     go(remote(mst.at[1], mrecv_y, mysem.at[0], mysem.at[1], other_y, x))
-    arrival(mrecv_y, mysem.at[0], mysem.at[1]).wait_recv()
-    msx[...] = mst[0] + mrecv_y[...]
-    for k in range(1, n):
-        go(remote(msx, mrecv_dp.at[k], msend.at[k], mrecv.at[k], me_y, to(k)))
-
-    mixed = msx[...]
-    for k in range(1, n):
-        arrival(mrecv_dp.at[k], msend.at[k], mrecv.at[k]).wait_recv()
-        mixed = mixed + mrecv_dp[k]
-    mix_ref[...] = mixed
-
     for k in range(1, n):
         block = rows(source(k) * own_rows, own_rows, own_rows)
         arrival(inv.at[block], isend.at[k], irecv.at[k]).wait_recv()
         arrival(lg.at[block], asend.at[k], arecv.at[k]).wait_recv()
     local[5].wait()
+
+    arrival(mrecv_y, mysem.at[0], mysem.at[1]).wait_recv()
+    msx[...] = mst[0] + mrecv_y[...]
+    for k in range(1, n):
+        go(remote(msx, mrecv_dp.at[k], msend.at[k], mrecv.at[k], me_y, to(k)))
 
     @pl.loop(0, tiles)
     def _(t):
@@ -485,6 +494,27 @@
         )
         gaing_ref[:, cols] = jnp.sum(norm_grad * scaled, axis=0, keepdims=True)
 
+    mixed = msx[...]
+    for k in range(1, n):
+        arrival(mrecv_dp.at[k], msend.at[k], mrecv.at[k]).wait_recv()
+        mixed = mixed + mrecv_dp[k]
+    sums = jnp.sum(mixed, axis=1, keepdims=True)
+    lane = lax.broadcasted_iota(jnp.int32, (1, MIXES), 1)
+
+    def mix_row(shift):
+        row = jnp.zeros((1, MIXES), F32)
+        for m in range(MIXES - shift):
+            row = jnp.where(lane == m, sums[m + shift : m + shift + 1, 0:1], row)
+        mix_ref[...] = row
+
+    @pl.when(h == 0)
+    def _():
+        mix_row(0)
+
+    @pl.when(h == 1)
+    def _():
+        mix_row(1)
+
     for copy in sends:
         copy.wait_send()
 
@@ -524,11 +554,6 @@
     feats = width // n
     tokens = own_rows * n
     chunks = tokens // 2 // CHUNK
-    side = (lax.axis_index("section") // stride) % 2
-    row = mix_weight[0]
-    zero = jnp.zeros((1,), F32)
-    rel = jnp.where(side == 1, jnp.concatenate([zero, row[:-1]]), row)
-    rel = jnp.broadcast_to(rel[:, None], (MIXES, 128))
     dma = pltpu.SemaphoreType.DMA
     anyspace = pl.BlockSpec(memory_space=pl.ANY)
     vmem = pl.BlockSpec(memory_space=pltpu.VMEM)
@@ -538,7 +563,7 @@
             jax.ShapeDtypeStruct((latents, feats), BF16),
             jax.ShapeDtypeStruct((feats, latents), BF16),
             jax.ShapeDtypeStruct((1, feats), F32),
-            jax.ShapeDtypeStruct((MIXES, 128), F32),
+            jax.ShapeDtypeStruct((1, MIXES), F32),
         ),
         in_specs=[anyspace] * 5 + [vmem] * 2,
         out_specs=(vmem,) * 4,
@@ -567,6 +592,7 @@
             pltpu.VMEM((own_rows, latents), F32),
             pltpu.VMEM((n, own_rows, latents), BF16),
             pltpu.VMEM((tokens, latents), BF16),
+            pltpu.VMEM((8, 128), F32),
             pltpu.VMEM((2, 8, 128), F32),
             pltpu.VMEM((2, tokens // 2, feats), BF16),
             pltpu.VMEM((16, 8, 128), F32),
@@ -596,10 +622,8 @@
         compiler_params=pltpu.CompilerParams(
             collective_id=0, has_side_effects=True, vmem_limit_bytes=60 * 1024 * 1024
         ),
-    )(layer_in[0], latent[0], mix_grad[0], down_proj[0], up_proj[0], norm_gain, rel)
-    sums = jnp.sum(mixed, axis=1)
-    mixing = jnp.where(side == 1, jnp.concatenate([sums[1:], zero]), sums)
-    return (up_grad[None], down_grad[None], gain_grad, mixing[None])
+    )(layer_in[0], latent[0], mix_grad[0], down_proj[0], up_proj[0], norm_gain, mix_weight)
+    return (up_grad[None], down_grad[None], gain_grad, mixed)
 
 
 def solution(mesh):

time: 110 us -> 104 us (0.945)
  Pallas kernels: 100 us -> 97.6 us
  other arithmetic: 2.12 us -> 0 us
    pallas_call x1, Pallas kernels: 100 us -> 97.6 us  [local(): pl.pallas_call(functools.partial(kernel, n, stride), out_shape=(jax.Shape...]
    select_n x2 -> x0, other arithmetic: 1.32 us -> none  [the longest x1 0.73 us: local(): rel = jnp.where(side == 1, jnp.concatenate([zero, row[:-1]]), row)]
    unnamed x7 -> x10, local copies, waits for them, and re-layouts: 4.96 us -> 5.48 us
where the time goes in v3:
time: 104 us
  Pallas kernels  97.6 us (94%)
  local copies, waits for them, and re-layouts  5.48 us (5%)
    pallas_call x1, Pallas kernels, local(): pl.pallas_call(functools.partial(kernel, n, stride), out_shape=(jax.Shape...  97.6 us
    unnamed x10, local copies, waits for them, and re-layouts  5.48 us

profile of v3, /device:TPU:0, one launch (start us, length us, event | category | flops | bytes accessed | tf_op | source)
XLA Modules:
  0.0 103.8 jit_solution(17557750706710934651)
XLA Ops:
  0.6 97.6 %shard_map.102 = (bf16[384,2560]{1,0:T(8,128)(2,1)}, bf16[2560,384]{1,0:T(8,128)(2,1)}, f32[1,2560]{1,0:T(1,128)}, f32[1,8]{1,0:T(1,128)}) custom-call(bf16[128,5120]{1,0:T(8,128)(2,1)} %bitcast.11, bf16[128,384]{1,0:T(8,128)(2,1)} %bitcast.13, bf16[128,5120]{1,0:T(8,128)(2,1)} %bitcast.12, bf16[2560,384]{1,0:T(8,128)(2,1)} %bitcast.7, ...), custom_call_target="tpu_custom_call" | custom-call | tf_op jit(solution)/shard_map/pallas_call | solution.py:560
  98.3 0.0 copy-start
  98.3 3.1 %copy.15 = bf16[1,384,2560]{2,1,0:T(8,128)(2,1)} copy(bf16[1,384,2560]{2,1,0:T(8,128)(2,1)} %bitcast.10) | data formatting | bytes 3932160
  101.4 0.0 copy-done
  101.4 0.0 copy-start.1
  101.4 0.0 copy-start.2
  101.4 1.3 %copy.16 = bf16[1,2560,384]{2,1,0:T(8,128)(2,1)} copy(bf16[1,2560,384]{2,1,0:T(8,128)(2,1)S(1)} %bitcast.9) | data formatting | bytes 3932160
  102.7 0.0 copy-done.1
  102.7 0.6 copy.17
  103.3 0.0 copy-done.2
  103.3 0.5 copy.18
Async XLA Ops:
  98.3 3.1 %copy-start = (bf16[2560,384]{1,0:T(8,128)(2,1)S(1)}, bf16[2560,384]{1,0:T(8,128)(2,1)}, u32[]{:S(2)}) copy-start(bf16[2560,384]{1,0:T(8,128)(2,1)} %get-tuple-element.9) | copy-start | bytes 5898244
  101.4 1.3 %copy-start.1 = (f32[1,2560]{1,0:T(1,128)S(1)}, f32[1,2560]{1,0:T(1,128)}, u32[]{:S(2)}) copy-start(f32[1,2560]{1,0:T(1,128)} %get-tuple-element.18) | copy-start | bytes 30724
  101.4 1.9 %copy-start.2 = (f32[1,8]{1,0:T(1,128)S(1)}, f32[1,8]{1,0:T(1,128)}, u32[]{:S(2)}) copy-start(f32[1,8]{1,0:T(1,128)} %get-tuple-element.19) | copy-start | bytes 100
